TPU v7x, 32 devices: a whole 2x2x4 slice. The times are simulated.
32 devices in a mesh: seq: 4 (over x, core), vocab: 8 (over z, y).
Axes of the slice: x: 2, y: 2, z: 4, core: 2. Of those that a mesh axis runs over, the one named last changes fastest.
Arguments:
- hidden: bfloat16 [512, 4608], P('seq', 'vocab'), may hold values from -6 to 6
- norm_gain: float32 [4608], replicated, may hold values from -1.5 to 1.5
- unembed: bfloat16 [256000, 4608], P(('seq', 'vocab')), may hold values from -0.375 to 0.375
- targets: int32 [512], P('seq'), may hold values from 0 to 255999
Outputs:
- log_prob: float32 [512], P('seq')
- entropy: float32 [512], P('seq')
All inputs are finite; a program needn't handle non-finite values.
Results may differ from a plain program's by a relative error of at most 0.0012.
Values may be sent and summed in bfloat16 or wider, within the bound.
A program may use at most 128 MiB of HBM per device.

v0:
```python
import functools

import jax
import jax.numpy as jnp
from jax import lax
from jax.experimental import pallas as pl
from jax.experimental.pallas import tpu as pltpu
from jax.sharding import PartitionSpec as P

softcap = 30.0
epsilon = 1e-06
CORES = 2
QUARTERS = 4
MESH = pl.DeviceIdType.MESH
ORDERS = (("x", "y", "z"), ("y", "x", "z"), ("z", "x", "y"), ("z", "y", "x"))


def gather_kernel(sizes, hidden_ref, gain_ref, targets_ref, normed_ref, all_targets_ref,
                  held, load_sem, send_sem, recv_sem, pair_send, pair_recv, id_send, id_recv):
    X, Y, Z = sizes["x"], sizes["y"], sizes["z"]
    seq, vocab = lax.axis_index("seq"), lax.axis_index("vocab")
    core = lax.rem(seq, CORES)
    me = {"x": seq // CORES, "y": lax.rem(vocab, Y), "z": vocab // Y}
    rows, part = held.shape[5], held.shape[6]

    def device(**moved):
        at = {**me, **moved}
        return {"seq": at["x"] * CORES + at.get("core", core), "vocab": at["z"] * Y + at["y"]}

    loads = [
        pltpu.make_async_copy(
            hidden_ref.at[pl.ds(q * rows, rows)],
            held.at[core, q, me["z"], me["y"], me["x"]],
            load_sem.at[q],
        )
        for q in range(QUARTERS)
    ]
    for load in loads:
        load.start()

    seqs = X * CORES
    greeted = [{"seq": lax.rem(seq + k, seqs), "vocab": vocab} for k in range(1, seqs)]
    for d in ("y", "z"):
        n = sizes[d]
        for k in sorted({1, n - 1}) if n > 1 else ():
            greeted.append(device(**{d: lax.rem(me[d] + k, n)}))
    barrier = pltpu.get_barrier_semaphore()
    for other in greeted:
        pl.semaphore_signal(barrier, inc=1, device_id=other, device_id_type=MESH)
    all_targets_ref[seq] = targets_ref[...]
    for load in loads:
        load.wait()
    pl.semaphore_wait(barrier, len(greeted))

    sends = []

    def targets_copy(k, to, slot):
        return pltpu.make_async_remote_copy(
            src_ref=targets_ref, dst_ref=all_targets_ref.at[slot],
            send_sem=id_send.at[k - 1], recv_sem=id_recv.at[k - 1],
            device_id={"seq": to, "vocab": vocab}, device_id_type=MESH,
        )

    def quarter(q):
        done = set()
        for axis, d in enumerate(ORDERS[q]):
            n = sizes[d]
            ahead = n // 2 if q % 2 == 0 else (n - 1) // 2
            behind = n - 1 - ahead

            def region(i):
                index = tuple(
                    i if e == d else (pl.ds(0, sizes[e]) if e in done else me[e]) for e in ("z", "y", "x")
                )
                return held.at[(core, q) + index]

            def copy(step, way):
                i = lax.rem(me[d] + (n - step + 1 if way == 0 else step - 1), n)
                sem = (q, axis, way, step - 1)
                return pltpu.make_async_remote_copy(
                    src_ref=region(i), dst_ref=region(i),
                    send_sem=send_sem.at[sem], recv_sem=recv_sem.at[sem],
                    device_id=device(**{d: lax.rem(me[d] + (1 if way == 0 else n - 1), n)}),
                    device_id_type=MESH,
                )

            for step in range(1, max(ahead, behind) + 1):
                going = [copy(step, w) for w, last in ((0, ahead), (1, behind)) if step <= last]
                for c in going:
                    c.start()
                sends.extend(going)
                yield
                for c in going:
                    c.wait_recv()
            done.add(d)
        pair = pltpu.make_async_remote_copy(
            src_ref=held.at[core, q], dst_ref=held.at[core, q],
            send_sem=pair_send.at[q], recv_sem=pair_recv.at[q],
            device_id=device(core=1 - core), device_id_type=MESH,
        )
        pair.start()
        sends.append(pair)
        pairs[q] = pair

    pairs = {}
    running = [quarter(q) for q in range(QUARTERS)]
    first = True
    while running:
        running = [g for g in running if next(g, "end") is None]
        if first:
            ids = [targets_copy(k, lax.rem(seq + k, seqs), seq) for k in range(1, seqs)]
            for c in ids:
                c.start()
            first = False
    for c in ids:
        c.wait()

    width = Z * Y * part
    for q in range(QUARTERS):
        pairs[q].wait_recv()

        def block(i, _, q=q):
            c, x = lax.rem(i, CORES), i // CORES
            squares = jnp.zeros((rows, 1), jnp.float32)
            for v in range(Z * Y):
                values = held[c, q, v // Y, v % Y, x].astype(jnp.float32)
                squares += jnp.sum(values * values, axis=1, keepdims=True)
            scale = lax.rsqrt(squares / width + epsilon)
            start = pl.multiple_of((x * CORES + c) * (rows * QUARTERS) + q * rows, rows)
            for v in range(Z * Y):
                values = held[c, q, v // Y, v % Y, x].astype(jnp.float32)
                normed_ref[pl.ds(start, rows), v * part:(v + 1) * part] = (
                    values * scale * (1.0 + gain_ref[v])
                ).astype(jnp.bfloat16)
            return 0

        lax.fori_loop(0, X * CORES, block, 0)
    for c in sends:
        c.wait_send()


def exchange_kernel(seqs, vocabs, stats_ref, log_prob_ref, entropy_ref, arrived, send_sem, recv_sem):
    count = seqs * vocabs
    seq, vocab = lax.axis_index("seq"), lax.axis_index("vocab")
    me = seq * vocabs + vocab

    def place(k):
        other = lax.rem(me + k, count)
        return other, {"seq": other // vocabs, "vocab": lax.rem(other, vocabs)}

    barrier = pltpu.get_barrier_semaphore()

    def greet(k, _):
        pl.semaphore_signal(barrier, inc=1, device_id=place(k)[1], device_id_type=MESH)
        return 0

    lax.fori_loop(1, count, greet, 0)
    arrived[me] = stats_ref[seq]
    pl.semaphore_wait(barrier, count - 1)

    def copy(k, slot):
        other, where = place(k)
        return pltpu.make_async_remote_copy(
            src_ref=stats_ref.at[other // vocabs], dst_ref=arrived.at[slot],
            send_sem=send_sem.at[k], recv_sem=recv_sem.at[slot],
            device_id=where, device_id_type=MESH,
        )

    def send(k, _):
        copy(k, me).start()
        return 0

    def sent(k, _):
        copy(k, me).wait_send()
        return 0

    def receive(k, _):
        copy(k, place(k)[0]).wait_recv()
        return 0

    lax.fori_loop(1, count, send, 0)
    lax.fori_loop(1, count, receive, 0)
    sums = arrived[0]
    for i in range(1, count):
        sums = sums + arrived[i]
    total, moment, chosen = sums[0:1], sums[1:2], sums[2:3]
    log_norm = softcap + jnp.log(total)
    log_prob_ref[...] = chosen - log_norm
    entropy_ref[...] = log_norm - moment / total
    lax.fori_loop(1, count, sent, 0)


def token_stats(logits, target_rows, first):
    capped = softcap * jnp.tanh(logits / softcap)
    weights = jnp.exp(capped - softcap)
    columns = first + lax.broadcasted_iota(jnp.int32, logits.shape, 1)
    chosen = jnp.where(columns == target_rows[:, None], capped, 0.0)
    return jnp.stack(
        [jnp.sum(weights, axis=1), jnp.sum(weights * capped, axis=1), jnp.sum(chosen, axis=1)]
    )


def on_device(seqs, vocabs, hidden, norm_gain, unembed, targets):
    vocab_rows, width = unembed.shape
    own, part = hidden.shape
    first = lax.axis_index(("seq", "vocab")) * vocab_rows
    Y = 2 ** ((vocabs.bit_length() - 1) // 2)
    sizes = {"x": seqs // CORES, "y": Y, "z": vocabs // Y}
    steps = max(max(n // 2 for n in sizes.values()), 1)
    vmem = pl.BlockSpec(memory_space=pltpu.VMEM)
    normed, all_targets = pl.pallas_call(
        functools.partial(gather_kernel, sizes),
        out_shape=(
            jax.ShapeDtypeStruct((seqs * own, width), jnp.bfloat16),
            jax.ShapeDtypeStruct((seqs, 1, own), jnp.int32),
        ),
        in_specs=[pl.BlockSpec(memory_space=pltpu.HBM), vmem, vmem],
        out_specs=(vmem, vmem),
        scratch_shapes=[
            pltpu.VMEM((CORES, QUARTERS, sizes["z"], Y, sizes["x"], own // QUARTERS, part), jnp.bfloat16),
            pltpu.SemaphoreType.DMA((QUARTERS,)),
            pltpu.SemaphoreType.DMA((QUARTERS, 3, 2, steps)),
            pltpu.SemaphoreType.DMA((QUARTERS, 3, 2, steps)),
            pltpu.SemaphoreType.DMA((QUARTERS,)),
            pltpu.SemaphoreType.DMA((QUARTERS,)),
            pltpu.SemaphoreType.DMA((seqs - 1,)),
            pltpu.SemaphoreType.DMA((seqs - 1,)),
        ],
        compiler_params=pltpu.CompilerParams(collective_id=0, has_side_effects=True),
        name="gather_norm",
    )(hidden, norm_gain.reshape(vocabs, 1, part), targets.reshape(1, own))
    logits = lax.dot_general(
        normed, unembed, (((1,), (1,)), ((), ())), preferred_element_type=jnp.float32
    )
    stats = token_stats(logits, all_targets.reshape(seqs * own), first)
    stats = jnp.transpose(stats.reshape(3, seqs, own), (1, 0, 2))
    log_prob, entropy = pl.pallas_call(
        functools.partial(exchange_kernel, seqs, vocabs),
        out_shape=(jax.ShapeDtypeStruct((1, own), jnp.float32),) * 2,
        in_specs=[vmem],
        out_specs=(vmem, vmem),
        scratch_shapes=[
            pltpu.VMEM((seqs * vocabs, 3, own), jnp.float32),
            pltpu.SemaphoreType.DMA((seqs * vocabs,)),
            pltpu.SemaphoreType.DMA((seqs * vocabs,)),
        ],
        compiler_params=pltpu.CompilerParams(collective_id=1, has_side_effects=True),
        name="exchange",
    )(stats)
    return log_prob.reshape(own), entropy.reshape(own)


def solution(mesh):
    return jax.shard_map(
        functools.partial(on_device, mesh.shape["seq"], mesh.shape["vocab"]),
        mesh=mesh,
        in_specs=(P("seq", "vocab"), P(), P(("seq", "vocab"), None), P("seq")),
        out_specs=(P("seq"), P("seq")),
        check_vma=False,
    )
```

profile of v0, /device:TPU:0, one launch (start us, length us, event | category | flops | bytes accessed | tf_op | source)
XLA Modules:
  0.0 110.0 jit_solution(2198318634981307641)
XLA Ops:
  0.6 1.7 %copy.6.hidden_ref = bf16[128,576]{1,0:T(8,128)(2,1)} copy(bf16[128,576]{0,1:T(8,128)(2,1)} %param.4) | data formatting | bytes 294912 | tf_op args[0]
  2.3 1.4 %reshape.24.gain_ref = f32[8,1,576]{2,1,0:T(1,128)} reshape(f32[4608]{0:T(1024)} %param.5) | data formatting | bytes 36864 | tf_op jit(solution)/shard_map/reshape | solution.py:231
  3.8 42.3 %gather_norm.1 = (bf16[512,4608]{1,0:T(8,128)(2,1)}, s32[4,1,128]{2,1,0:T(1,128)}) custom-call(bf16[128,576]{1,0:T(8,128)(2,1)} %copy.6.hidden_ref, f32[8,1,576]{2,1,0:T(1,128)} %reshape.24.gain_ref, s32[1,128]{1,0:T(1,128)} %bitcast.14), custom_call_target="tpu_custom_call" | custom-call | tf_op jit(solution)/shard_map/gather_norm/pallas_call | solution.py:211
  46.1 50.2 %fusion = (f32[512]{0:T(512)S(1)}, f32[512]{0:T(512)S(1)}, f32[512]{0:T(512)S(1)}) fusion(s32[512]{0:T(512)} %bitcast.15, s32[8000]{0:T(1024)S(1)} %iota_add_fusion, bf16[512,4608]{1,0:T(8,128)(2,1)} %get-tuple-element.6, bf16[8000,4608]{1,0:T(8,128)(2,1)} %param.6), kind=kOutput, calls=%fused_computation.3 | convolution fusion | flops 37785600000 | bytes 78486784 | tf_op jit(solution)/shard_map/dot_general | solution.py:232
  96.3 0.6 maximum_bitcast_fusion.stats_ref
  96.9 10.8 %exchange.1 = (f32[1,128]{1,0:T(1,128)}, f32[1,128]{1,0:T(1,128)}) custom-call(f32[4,3,128]{2,1,0:T(4,128)} %maximum_bitcast_fusion.stats_ref), custom_call_target="tpu_custom_call" | custom-call | tf_op jit(solution)/shard_map/exchange/pallas_call | solution.py:237
  107.7 1.1 %copy.9 = f32[128]{0:T(128)} copy(f32[128]{0:T(128)} %bitcast.17) | data formatting | bytes 1024
  108.8 1.1 %copy.10 = f32[128]{0:T(128)} copy(f32[128]{0:T(128)} %bitcast.16) | data formatting | bytes 1024
  (1 shorter events, 0.0 us)
where the time goes:
time: 110 us
  Pallas kernels  53.1 us (48%)
  matrix products  50.2 us (46%)
  local copies, waits for them, and re-layouts  5.37 us (5%)
    dot_general x1, matrix products, on_device(): lax.dot_general(normed, unembed, (((1,), (1,)), ((), ())), preferred_elem...  50.2 us
    pallas_call x1, Pallas kernels, on_device(): pl.pallas_call(functools.partial(gather_kernel, sizes), out_shape=(jax.Sh...  42.3 us
    pallas_call x1, Pallas kernels, on_device(): pl.pallas_call(functools.partial(exchange_kernel, seqs, vocabs), out_shap...  10.8 us
    unnamed x3, local copies, waits for them, and re-layouts  3.96 us

commit v1 on v0

v1 whole, which is shorter than its diff:
```python
import functools

import jax
import jax.numpy as jnp
from jax import lax
from jax.experimental import pallas as pl
from jax.experimental.pallas import tpu as pltpu
from jax.sharding import PartitionSpec as P

softcap = 30.0
epsilon = 1e-06
log2e = 1.4426950408889634
CORES = 2
LANES = 128
DEPTH = 256
SLOTS = 3
MESH = pl.DeviceIdType.MESH


def divisor(extent, most):
    return max(n for n in range(16, most + 1, 16) if extent % n == 0)


def plan(stages, chunk):
    whole = chunk // DEPTH * DEPTH
    passes = [[(0, 0, whole)]]
    if stages > 1:
        passes.append([(0, whole, chunk - whole), (1, 0, chunk)])
    elif whole < chunk:
        passes.append([(0, whole, chunk - whole)])
    if stages > 2:
        passes.append([(k, 0, chunk) for k in range(2, stages)])
    return [[piece for piece in part if piece[2]] for part in passes]


def head_kernel(sizes, tile, sub, hidden_ref, gain_ref, targets_ref, unembed_ref, out_ref,
                held, gains, normed, partial, scales, all_targets, weights, logits, sums,
                stats, arrived, sems, weight_sem):
    X, Y, Z = sizes["x"], sizes["y"], sizes["z"]
    seq, vocab = lax.axis_index("seq"), lax.axis_index("vocab")
    core = lax.rem(seq, CORES)
    x, y, z = seq // CORES, lax.rem(vocab, Y), vocab // Y
    seqs, vocabs = X * CORES, Z * Y
    count = seqs * vocabs
    me = seq * vocabs + vocab
    part, own = held.shape[4], held.shape[5]
    chunk, width, tokens = Y * part, Z * Y * part, seqs * own
    rows = unembed_ref.shape[0]
    tiles = rows // tile
    passes = plan(Z, chunk)
    total_steps = len(passes) * tiles

    def place(k):
        other = lax.rem(me + k, count)
        return other, {"seq": other // vocabs, "vocab": lax.rem(other, vocabs)}

    def device(dx=0, dy=0, dz=0, dc=0):
        return {
            "seq": lax.rem(x + dx, X) * CORES + lax.rem(core + dc, CORES),
            "vocab": lax.rem(z + dz, Z) * Y + lax.rem(y + dy, Y),
        }

    def level(k):
        return lax.rem(z - k + Z, Z)

    barrier = pltpu.get_barrier_semaphore()

    def greet(k, _):
        pl.semaphore_signal(barrier, inc=1, device_id=place(k)[1], device_id_type=MESH)
        return 0

    lax.fori_loop(1, count, greet, 0)

    def fetches(p, i, slot):
        start, out = 0, []
        row = pl.ds(pl.multiple_of(i * tile, tile), tile)
        for n, (k, first, length) in enumerate(passes[p]):
            column = pl.multiple_of(level(k) * chunk + first, LANES)
            out.append(pltpu.make_async_copy(
                unembed_ref.at[row, pl.ds(column, length)],
                weights.at[slot, :, pl.ds(start, length)],
                weight_sem.at[slot, n],
            ))
            start += length
        return out

    for g in range(min(SLOTS - 1, total_steps)):
        for copy in fetches(g // tiles, g % tiles, g % SLOTS):
            copy.start()

    squares = jnp.zeros((1, own), jnp.float32)
    for a in range(0, part, LANES):
        b = min(a + LANES, part)
        values = jnp.transpose(hidden_ref[:, a:b].astype(jnp.float32))
        squares += jnp.sum(values * values, axis=0, keepdims=True)
        held[core, z, x, y, a:b, :] = values.astype(jnp.bfloat16)
    partial[me] = squares
    all_targets[seq] = targets_ref[...]
    pl.semaphore_wait(barrier, count - 1)

    def remote(src, dst, name, index, to):
        return pltpu.make_async_remote_copy(
            src_ref=src, dst_ref=dst, send_sem=sems[name].at[(0,) + index],
            recv_sem=sems[name].at[(1,) + index], device_id=to, device_id_type=MESH,
        )

    def square_copy(k, slot):
        return remote(partial.at[slot], partial.at[slot], "square", (k,), place(k)[1])

    def target_copy(k, slot):
        return remote(targets_ref, all_targets.at[slot], "target", (k,),
                      {"seq": lax.rem(seq + k, seqs), "vocab": vocab})

    peers = sorted(
        ((dx, dy) for dx in range(X) for dy in range(Y) if dx or dy),
        key=lambda d: (d[0] != 0) + (d[1] != 0),
    )

    def plane_copy(k, j, sx, sy):
        block = held.at[core, level(k), sx, sy]
        dx, dy = peers[j]
        return remote(block, block, "plane", (k, j), device(dx=dx, dy=dy))

    def plane_send(k, j):
        return plane_copy(k, j, x, y)

    def plane_recv(k, j):
        dx, dy = peers[j]
        return plane_copy(k, j, lax.rem(x - dx + X, X), lax.rem(y - dy + Y, Y))

    def column_copy(k, level_):
        block = held.at[core, level_, x, y]
        return remote(block, block, "column", (k,), device(dz=k))

    def pair_copy(k, j, mine):
        dx, dy = (0, 0) if j == len(peers) else peers[j]
        c = core if mine else 1 - core
        block = held.at[c, level(k), lax.rem(x - dx + X, X), lax.rem(y - dy + Y, Y)]
        return remote(block, block, "pair", (k, j), device(dc=1))

    def send_square(k, _):
        square_copy(k, me).start()
        return 0

    lax.fori_loop(1, count, send_square, 0)
    for k in range(1, seqs):
        target_copy(k, seq).start()

    def spread(k):
        for j in range(len(peers)):
            plane_send(k, j).start()
        pair_copy(k, len(peers), True).start()

    def column_arrived(k):
        column_copy(k, level(k)).wait_recv()
        spread(k)

    def plane_arrived(k):
        for j in range(len(peers)):
            plane_recv(k, j).wait_recv()
            pair_copy(k, j, True).start()

    def pair_arrived(k):
        for j in range(len(peers) + 1):
            pair_copy(k, j, False).wait_recv()

    spread(0)
    for k in range(1, Z):
        column_copy(k, z).start()

    lanes = width // LANES
    columns = jnp.transpose(jnp.concatenate(
        [1.0 + gain_ref[...], jnp.zeros((LANES - lanes, LANES), jnp.float32)], axis=0
    ))
    for j in range(lanes):
        gains[j * LANES:(j + 1) * LANES, :] = jnp.broadcast_to(columns[:, j:j + 1], (LANES, LANES))

    def square_arrived(k, _):
        square_copy(k, place(count - k)[0]).wait_recv()
        return 0

    lax.fori_loop(1, count, square_arrived, 0)
    for s in range(seqs):
        squares = partial[s * vocabs]
        for v in range(1, vocabs):
            squares = squares + partial[s * vocabs + v]
        scales[s] = lax.rsqrt(squares / width + epsilon)
    for k in range(1, seqs):
        target_copy(k, lax.rem(seq - k + seqs, seqs)).wait_recv()

    def normalize(k):
        for s in range(seqs):
            for v in range(Y):
                block = held[s % CORES, level(k), s // CORES, v].astype(jnp.float32)
                start = pl.multiple_of(level(k) * chunk + v * part, 16)
                at = k * chunk + v * part
                normed[at:at + part, s * own:(s + 1) * own] = (
                    block * scales[s] * gains[pl.ds(start, part), :]
                ).astype(jnp.bfloat16)

    plane_arrived(0)
    pair_arrived(0)
    normalize(0)

    ids = jnp.concatenate([all_targets[s] for s in range(seqs)], axis=1) - me * rows
    lines = lax.broadcasted_iota(jnp.int32, (sub, tokens), 0)
    sums[...] = jnp.zeros_like(sums)

    def fold(values):
        return jnp.sum(values.reshape(sub // 8, 8, tokens), axis=0)

    events = [[] for _ in passes]
    last_pass = len(passes) - 1
    if Z > 1:
        early = [(functools.partial(column_arrived, k)) for k in range(1, Z)]
        for n, event in enumerate(early):
            events[0].append((min(n, tiles - 1), event))
        events[0].append((tiles - 1, functools.partial(plane_arrived, 1)))
        for n, k in enumerate(range(2, Z)):
            events[1].append((min(1 + 2 * n, tiles - 1), functools.partial(plane_arrived, k)))

    base = 0
    for p, pieces in enumerate(passes):
        depth = sum(length for _, _, length in pieces)
        for k in sorted({piece[0] for piece in pieces}):
            if k and pieces[-1][0] >= k and (p == 0 or k not in {q[0] for q in passes[p - 1]}):
                pair_arrived(k)
                normalize(k)

        def step(i, _, p=p, depth=depth, base=base):
            g = p * tiles + i
            slot = lax.rem(g, SLOTS)
            ahead = lax.rem(g + SLOTS - 1, SLOTS)

            def prefetch(q, n):
                for copy in fetches(q, n, ahead):
                    copy.start()

            n = i + SLOTS - 1
            for q in range(p, len(passes)):
                low, high = (q - p) * tiles, (q - p + 1) * tiles
                if low > tiles - 1 + SLOTS - 1 or high <= SLOTS - 1:
                    continue
                pl.when((n >= low) & (n < high))(functools.partial(prefetch, q, n - low))
            for at, event in events[p]:
                pl.when(i == at)(event)
            for copy in fetches(p, i, slot):
                copy.wait()
            if p == last_pass:
                total, moment, chosen = sums[0], sums[1], sums[2]
            for s in range(tile // sub):
                here = pl.ds(pl.multiple_of(i * tile + s * sub, sub), sub)
                value = jnp.dot(
                    weights[slot, s * sub:(s + 1) * sub, 0:depth], normed[base:base + depth, :],
                    preferred_element_type=jnp.float32,
                )
                if p:
                    value = logits[here, :] + value
                if p < last_pass:
                    logits[here, :] = value
                else:
                    squashed = jnp.tanh(value * (1.0 / softcap))
                    weight = jnp.exp2(squashed * (softcap * log2e) - softcap * log2e)
                    hit = lines == ids - (i * tile + s * sub)
                    total = total + fold(weight)
                    moment = moment + fold(weight * squashed)
                    chosen = chosen + fold(jnp.where(hit, squashed, 0.0))
            if p == last_pass:
                sums[0], sums[1], sums[2] = total, moment, chosen
            return 0

        lax.fori_loop(0, tiles, step, 0)
        base += depth

    line = jnp.concatenate([
        jnp.sum(sums[0], axis=0, keepdims=True),
        softcap * jnp.sum(sums[1], axis=0, keepdims=True),
        softcap * jnp.sum(sums[2], axis=0, keepdims=True),
    ], axis=0)
    for s in range(seqs):
        stats[s] = line[:, s * own:(s + 1) * own]
    arrived[me] = stats[seq]

    def square_sent(k, _):
        square_copy(k, me).wait_send()
        return 0

    lax.fori_loop(1, count, square_sent, 0)
    for k in range(1, seqs):
        target_copy(k, seq).wait_send()
    for k in range(Z):
        for j in range(len(peers)):
            plane_send(k, j).wait_send()
            pair_copy(k, j, True).wait_send()
        pair_copy(k, len(peers), True).wait_send()
        if k:
            column_copy(k, z).wait_send()

    def stat_copy(k, slot):
        other, where = place(k)
        return remote(stats.at[other // vocabs], arrived.at[slot], "stat", (k,), where)

    def send_stat(k, _):
        stat_copy(k, me).start()
        return 0

    def stat_arrived(k, _):
        stat_copy(k, place(count - k)[0]).wait_recv()
        return 0

    def stat_sent(k, _):
        stat_copy(k, me).wait_send()
        return 0

    lax.fori_loop(1, count, send_stat, 0)
    lax.fori_loop(1, count, stat_arrived, 0)
    result = arrived[0]
    for i in range(1, count):
        result = result + arrived[i]
    total, moment, chosen = result[0:1], result[1:2], result[2:3]
    log_norm = softcap + jnp.log(total)
    out_ref[0:1, :] = chosen - log_norm
    out_ref[1:2, :] = log_norm - moment / total
    lax.fori_loop(1, count, stat_sent, 0)


def on_device(seqs, vocabs, hidden, norm_gain, unembed, targets):
    rows, width = unembed.shape
    own, part = hidden.shape
    Y = 2 ** ((vocabs.bit_length() - 1) // 2)
    X, Z = seqs // CORES, vocabs // Y
    sizes = {"x": X, "y": Y, "z": Z}
    count = seqs * vocabs
    tokens = seqs * own
    tile = divisor(rows, 1600)
    sub = divisor(tile, 160)
    passes = plan(Z, Y * part)
    deepest = max(sum(length for _, _, length in pieces) for pieces in passes)
    most = max(len(pieces) for pieces in passes)
    planes = X * Y
    dma = pltpu.SemaphoreType.DMA
    vmem = pl.BlockSpec(memory_space=pltpu.VMEM)
    out = pl.pallas_call(
        functools.partial(head_kernel, sizes, tile, sub),
        out_shape=jax.ShapeDtypeStruct((2, own), jnp.float32),
        in_specs=[vmem, vmem, vmem, pl.BlockSpec(memory_space=pltpu.HBM)],
        out_specs=vmem,
        scratch_shapes=[
            pltpu.VMEM((CORES, Z, X, Y, part, own), jnp.bfloat16),
            pltpu.VMEM((width, LANES), jnp.float32),
            pltpu.VMEM((width, tokens), jnp.bfloat16),
            pltpu.VMEM((count, 1, own), jnp.float32),
            pltpu.VMEM((seqs, 1, own), jnp.float32),
            pltpu.VMEM((seqs, 1, own), jnp.int32),
            pltpu.VMEM((SLOTS, tile, deepest), jnp.bfloat16),
            pltpu.VMEM((rows, tokens), jnp.float32),
            pltpu.VMEM((3, 8, tokens), jnp.float32),
            pltpu.VMEM((seqs, 3, own), jnp.float32),
            pltpu.VMEM((count, 3, own), jnp.float32),
            {
                "square": dma((2, count)),
                "target": dma((2, seqs)),
                "plane": dma((2, Z, planes)),
                "column": dma((2, Z)),
                "pair": dma((2, Z, planes)),
                "stat": dma((2, count)),
            },
            dma((SLOTS, most)),
        ],
        compiler_params=pltpu.CompilerParams(
            collective_id=0, has_side_effects=True, vmem_limit_bytes=67000000
        ),
        name="head",
    )(hidden, norm_gain.reshape(width // LANES, LANES), targets.reshape(1, own), unembed)
    return out[0], out[1]


def solution(mesh):
    return jax.shard_map(
        functools.partial(on_device, mesh.shape["seq"], mesh.shape["vocab"]),
        mesh=mesh,
        in_specs=(P("seq", "vocab"), P(), P(("seq", "vocab"), None), P("seq")),
        out_specs=(P("seq"), P("seq")),
        check_vma=False,
    )
```

time: 110 us -> 78.1 us (0.71)
  matrix products: 50.2 us -> 0 us
  Pallas kernels: 53.1 us -> 74.4 us
  local copies, waits for them, and re-layouts: 5.37 us -> 2.94 us
    dot_general x1 -> x0, matrix products: 50.2 us -> none  [on_device(): lax.dot_general(normed, unembed, (((1,), (1,)), ((), ())), preferred_elem...]
    pallas_call x2 -> x1, Pallas kernels: 53.1 us -> 74.4 us  [on_device(): pl.pallas_call(functools.partial(head_kernel, sizes, tile, sub), out_shap...]
    unnamed x3 -> x1, local copies, waits for them, and re-layouts: 3.96 us -> 1.71 us
    reshape x1 -> x0, local copies, waits for them, and re-layouts: 1.41 us -> none  [on_device(): norm_gain.reshape(vocabs, 1, part)]
    squeeze x0 -> x1, local copies, waits for them, and re-layouts: none -> 1.23 us  [on_device(): return (out[0], out[1])]
where the time goes in v1:
time: 78.1 us; the launch traced here: 78 us
  Pallas kernels  74.4 us (95%)
  local copies, waits for them, and re-layouts  2.94 us (4%)
    pallas_call x1, Pallas kernels, on_device(): pl.pallas_call(functools.partial(head_kernel, sizes, tile, sub), out_shap...  74.4 us
    unnamed x1, local copies, waits for them, and re-layouts  1.71 us

profile of v1, /device:TPU:0, one launch (start us, length us, event | category | flops | bytes accessed | tf_op | source)
XLA Modules:
  0.0 78.0 jit_solution(7122502636886465348)
XLA Ops:
  0.6 1.7 %copy.6.hidden_ref = bf16[128,576]{1,0:T(8,128)(2,1)} copy(bf16[128,576]{0,1:T(8,128)(2,1)} %param.4) | data formatting | bytes 294912 | tf_op args[0]
  2.3 74.4 %head.1 = f32[2,128]{1,0:T(2,128)} custom-call(bf16[128,576]{1,0:T(8,128)(2,1)} %copy.6.hidden_ref, f32[36,128]{1,0:T(8,128)} %bitcast.6, s32[1,128]{1,0:T(1,128)} %bitcast.7, bf16[8000,4608]{1,0:T(8,128)(2,1)} %unembed_ref.1), custom_call_target="tpu_custom_call" | custom-call | tf_op jit(solution)/shard_map/head/pallas_call | solution.py:343
  76.7 1.2 %slice_bitcast_fusion = (f32[128]{0:T(128)}, f32[128]{0:T(128)}) fusion(f32[2,128]{1,0:T(2,128)} %head.1), kind=kLoop, calls=%fused_computation | loop fusion | bytes 2048 | tf_op jit(solution)/shard_map/squeeze | solution.py:375

commit v2 on v1

v2 whole, which is shorter than its diff:
```python
import functools

import jax
import jax.numpy as jnp
from jax import lax
from jax.experimental import pallas as pl
from jax.experimental.pallas import tpu as pltpu
from jax.sharding import PartitionSpec as P

softcap = 30.0
epsilon = 1e-06
log2e = 1.4426950408889634
CORES = 2
LANES = 128
DEPTH = 256
SLOTS = 3
MESH = pl.DeviceIdType.MESH


def divisor(extent, most):
    return max(n for n in range(16, most + 1, 16) if extent % n == 0)


def plan(stages, parts, part):
    chunk = parts * part
    own = part // DEPTH * DEPTH
    if parts == 2 and own and (part - own) % (LANES // 2) == 0:
        passes = [[(0, "own", own)], [(0, "rest", own)]]
        left = [(0, "left", chunk - 2 * own)]
    else:
        own = chunk // DEPTH * DEPTH
        passes = [[(0, "own", own)]]
        left = [(0, "rest", chunk - own)]
    left = [piece for piece in left if piece[2]]
    if stages > 1:
        passes.append(left + [(1, 0, chunk)])
    elif left:
        passes.append(left)
    if stages > 2:
        passes.append([(k, 0, chunk) for k in range(2, stages)])
    return passes


def chunk_gap(passes):
    return sum(piece[2] for pieces in passes for piece in pieces if piece[1] == "left")


def head_kernel(sizes, tile, sub, wide, wide_sub, hidden_ref, gain_hbm, targets_hbm, unembed_ref, out_ref,
                held, gain_ref, targets_ref, gains, normed, partial, scales, all_targets, weights, wides, logits, sums,
                stats, arrived, sems, weight_sem, wide_sem, load_sem):
    X, Y, Z = sizes["x"], sizes["y"], sizes["z"]
    seq, vocab = lax.axis_index("seq"), lax.axis_index("vocab")
    core = lax.rem(seq, CORES)
    x, y, z = seq // CORES, lax.rem(vocab, Y), vocab // Y
    seqs, vocabs = X * CORES, Z * Y
    count = seqs * vocabs
    me = seq * vocabs + vocab
    part, own = held.shape[4], held.shape[5]
    chunk, width, tokens = Y * part, Z * Y * part, seqs * own
    rows = unembed_ref.shape[0]
    passes = plan(Z, Y, part)
    split = [piece[1] for pieces in passes for piece in pieces].count("left") > 0
    halves = 2 if split else 1
    narrow, tiles, broad = passes[halves:], rows // tile, rows // wide
    total_steps = len(narrow) * tiles
    lead = passes[0][0][2]
    rest = chunk - lead

    others = [(a, b) for a in range(seqs) for b in range(vocabs) if a or b]

    def place(a, b):
        return {"seq": lax.rem(seq + a, seqs), "vocab": lax.rem(vocab + b, vocabs)}

    def device(dx=0, dy=0, dz=0, dc=0):
        return {
            "seq": lax.rem(x + dx, X) * CORES + lax.rem(core + dc, CORES),
            "vocab": lax.rem(z + dz, Z) * Y + lax.rem(y + dy, Y),
        }

    def level(k):
        return lax.rem(z - k + Z, Z)

    barrier = pltpu.get_barrier_semaphore()

    loads = [
        pltpu.make_async_copy(src, dst, load_sem.at[n])
        for n, (src, dst) in enumerate((
            (hidden_ref, held.at[core, z, x, y]), (targets_hbm, targets_ref), (gain_hbm, gain_ref)
        ))
    ]
    for load in loads:
        load.start()
    for other in others:
        pl.semaphore_signal(barrier, inc=1, device_id=place(*other), device_id_type=MESH)

    def first_of(kind):
        if not split:
            return {"own": 0, "rest": lead}.get(kind, 0)
        behind = (1 - y) * lead
        return {"own": y * rest, "rest": behind, "left": behind + lead}.get(kind, 0)

    def wide_fetch(p, i):
        column = pl.multiple_of(level(0) * chunk + first_of(passes[p][0][1]), LANES)
        slot = i % wides.shape[0]
        return pltpu.make_async_copy(
            unembed_ref.at[pl.ds(i * wide, wide), pl.ds(column, lead)],
            wides.at[slot], wide_sem.at[slot],
        )

    def fetches(p, i, slot):
        start, out = 0, []
        row = pl.ds(pl.multiple_of(i * tile, tile), tile)
        for n, (k, first, length) in enumerate(narrow[p]):
            column = pl.multiple_of(level(k) * chunk + first_of(first), LANES)
            out.append(pltpu.make_async_copy(
                unembed_ref.at[row, pl.ds(column, length)],
                weights.at[slot, :, pl.ds(start, length)],
                weight_sem.at[slot, n],
            ))
            start += length
        return out

    bulk = [(p, i) for p in range(halves) for i in range(broad)]
    for p, i in bulk[:wides.shape[0]]:
        wide_fetch(p, i).start()
    for g in range(min(SLOTS - 1, total_steps)):
        for copy in fetches(g // tiles, g % tiles, g % SLOTS):
            copy.start()

    for load in loads:
        load.wait()
    all_targets[seq] = targets_ref[...]
    values = held[core, z, x, y].astype(jnp.float32)
    partial[me] = jnp.sum(values * values, axis=0, keepdims=True)
    pl.semaphore_wait(barrier, count - 1)

    def remote(src, dst, name, index, to):
        return pltpu.make_async_remote_copy(
            src_ref=src, dst_ref=dst, send_sem=sems[name].at[(0,) + index],
            recv_sem=sems[name].at[(1,) + index], device_id=to, device_id_type=MESH,
        )

    def square_copy(block, to):
        return remote(block, block, "square", (), to)

    square_all = square_copy(partial.at[pl.ds(0, count - 1)], place(*others[0]))

    def target_copy(k, slot):
        return remote(targets_ref, all_targets.at[slot], "target", (k,),
                      {"seq": lax.rem(seq + k, seqs), "vocab": vocab})

    peers = sorted(
        ((dx, dy) for dx in range(X) for dy in range(Y) if dx or dy),
        key=lambda d: (d[1] != 0, (d[0] != 0) + (d[1] != 0)),
    )

    def plane_copy(k, j, sx, sy):
        block = held.at[core, level(k), sx, sy]
        dx, dy = peers[j]
        return remote(block, block, "plane", (k, j), device(dx=dx, dy=dy))

    def plane_send(k, j):
        return plane_copy(k, j, x, y)

    def plane_recv(k, j):
        dx, dy = peers[j]
        return plane_copy(k, j, lax.rem(x - dx + X, X), lax.rem(y - dy + Y, Y))

    def column_copy(k, level_):
        block = held.at[core, level_, x, y]
        return remote(block, block, "column", (k,), device(dz=k))

    def pair_copy(k, j, mine):
        dx, dy = (0, 0) if j == len(peers) else peers[j]
        c = core if mine else 1 - core
        block = held.at[c, level(k), lax.rem(x - dx + X, X), lax.rem(y - dy + Y, Y)]
        return remote(block, block, "pair", (k, j), device(dc=1))

    for other in others:
        square_copy(partial.at[me], place(*other)).start()
    for k in range(1, seqs):
        target_copy(k, seq).start()

    def spread(k):
        for j in range(len(peers)):
            plane_send(k, j).start()
        pair_copy(k, len(peers), True).start()

    def column_arrived(k):
        column_copy(k, level(k)).wait_recv()
        spread(k)

    near = [j for j, d in enumerate(peers) if d[1] == 0]
    far = [j for j, d in enumerate(peers) if d[1] != 0]

    def plane_arrived(k, which=near + far):
        for j in which:
            plane_recv(k, j).wait_recv()
            pair_copy(k, j, True).start()

    def pair_arrived(k, which=near + far + [len(peers)]):
        for j in which:
            pair_copy(k, j, False).wait_recv()

    spread(0)
    for k in range(1, min(Z, 2)):
        column_copy(k, z).start()

    lanes = width // LANES
    columns = jnp.transpose(jnp.concatenate(
        [1.0 + gain_ref[...], jnp.zeros((LANES - lanes, LANES), jnp.float32)], axis=0
    ))
    for j in range(lanes):
        gains[j * LANES:(j + 1) * LANES, :] = jnp.broadcast_to(columns[:, j:j + 1], (LANES, LANES))

    square_all.wait_recv()
    for s in range(seqs):
        squares = partial[s * vocabs]
        for v in range(1, vocabs):
            squares = squares + partial[s * vocabs + v]
        scales[s] = lax.rsqrt(squares / width + epsilon)
    for k in range(2, min(Z, 3)):
        column_copy(k, z).start()
    for k in range(1, seqs):
        target_copy(k, lax.rem(seq - k + seqs, seqs)).wait_recv()

    gap = 0 if not split else rest - lead

    def normalize(k, offsets=range(Y)):
        for d in offsets:
            v = lax.rem(y + d, Y)
            for s in range(seqs):
                block = held[s % CORES, level(k), s // CORES, v].astype(jnp.float32)
                start = pl.multiple_of(level(k) * chunk + v * part, 16)
                at = pl.multiple_of(k * chunk + (gap if k else 0) + v * part, 16)
                normed[pl.ds(at, part), s * own:(s + 1) * own] = (
                    block * scales[s] * gains[pl.ds(start, part), :]
                ).astype(jnp.bfloat16)

    def far_arrived():
        plane_arrived(0, far)

    plane_arrived(0, near)
    if Z > 1:
        column_arrived(1)
    pair_arrived(0, near + [len(peers)])
    normalize(0, (0,))
    if not split:
        far_arrived()
        pair_arrived(0, far)
        normalize(0, range(1, Y))

    ids = jnp.concatenate([all_targets[s] for s in range(seqs)], axis=1) - me * rows
    lines = lax.broadcasted_iota(jnp.int32, (sub, tokens), 0)
    sums[...] = jnp.zeros_like(sums)

    for n, (p, i) in enumerate(bulk):
        slot = i % wides.shape[0]
        if split and (p, i) == (1, 0):
            pair_arrived(0, far)
            normalize(0, range(1, Y))
            normed[chunk:chunk + gap, :] = normed[
                pl.ds(pl.multiple_of(first_of("left"), 16), gap), :
            ]
        wide_fetch(p, i).wait()
        start = pl.multiple_of(first_of(passes[p][0][1]), 16)
        for s in range(wide // wide_sub):
            here = pl.ds(i * wide + s * wide_sub, wide_sub)
            value = jnp.dot(
                wides[slot, s * wide_sub:(s + 1) * wide_sub, :], normed[pl.ds(start, lead), :],
                preferred_element_type=jnp.float32,
            )
            logits[here, :] = logits[here, :] + value if p else value
        if n + wides.shape[0] < len(bulk):
            wide_fetch(*bulk[n + wides.shape[0]]).start()
        if split and n == 0:
            far_arrived()
        if n == min(1, len(bulk) - 1):
            for k in range(3, Z):
                column_copy(k, z).start()
        if n == min(2, len(bulk) - 1) and Z > 2:
            column_arrived(2)
        if n == min(2, len(bulk) - 1) and Z > 1:
            plane_arrived(1, near)
    if Z > 1:
        plane_arrived(1, far)

    def fold(values):
        return jnp.sum(values.reshape(sub // 8, 8, tokens), axis=0)

    events = [[] for _ in narrow]
    last_pass = len(narrow) - 1
    for k in range(3, Z):
        events[0].append((0, functools.partial(column_arrived, k)))
    for n, k in enumerate(range(2, Z)):
        events[0].append((min(tiles - 2 + n, tiles - 1), functools.partial(plane_arrived, k)))

    base = chunk if split else lead
    for p, pieces in enumerate(narrow):
        depth = sum(length for _, _, length in pieces)
        for k in sorted({piece[0] for piece in pieces}):
            if k:
                pair_arrived(k)
                normalize(k)

        def step(i, _, p=p, depth=depth, base=base):
            g = p * tiles + i
            slot = lax.rem(g, SLOTS)
            ahead = lax.rem(g + SLOTS - 1, SLOTS)

            def prefetch(q, n):
                for copy in fetches(q, n, ahead):
                    copy.start()

            n = i + SLOTS - 1
            for q in range(p, len(narrow)):
                low, high = (q - p) * tiles, (q - p + 1) * tiles
                if low > tiles - 1 + SLOTS - 1 or high <= SLOTS - 1:
                    continue
                pl.when((n >= low) & (n < high))(functools.partial(prefetch, q, n - low))
            for at, event in events[p]:
                pl.when(i == at)(event)
            for copy in fetches(p, i, slot):
                copy.wait()
            if p == last_pass:
                total, moment, chosen = sums[0], sums[1], sums[2]
            for s in range(tile // sub):
                here = pl.ds(pl.multiple_of(i * tile + s * sub, sub), sub)
                value = jnp.dot(
                    weights[slot, s * sub:(s + 1) * sub, 0:depth], normed[base:base + depth, :],
                    preferred_element_type=jnp.float32,
                )
                value = logits[here, :] + value
                if p < last_pass:
                    logits[here, :] = value
                else:
                    squashed = jnp.tanh(value * (1.0 / softcap))
                    weight = jnp.exp2(squashed * (softcap * log2e) - softcap * log2e)
                    hit = lines == ids - (i * tile + s * sub)
                    total = total + fold(weight)
                    moment = moment + fold(weight * squashed)
                    chosen = chosen + fold(jnp.where(hit, squashed, 0.0))
            if p == last_pass:
                sums[0], sums[1], sums[2] = total, moment, chosen
            return 0

        lax.fori_loop(0, tiles, step, 0)
        base += depth

    line = jnp.concatenate([
        jnp.sum(sums[0], axis=0, keepdims=True),
        softcap * jnp.sum(sums[1], axis=0, keepdims=True),
        softcap * jnp.sum(sums[2], axis=0, keepdims=True),
    ], axis=0)
    for s in range(seqs):
        stats[s] = line[:, s * own:(s + 1) * own]
    arrived[me] = stats[seq]

    square_all.wait_send()
    for k in range(1, seqs):
        target_copy(k, seq).wait_send()
    for k in range(Z):
        for j in range(len(peers)):
            plane_send(k, j).wait_send()
            pair_copy(k, j, True).wait_send()
        pair_copy(k, len(peers), True).wait_send()
        if k:
            column_copy(k, z).wait_send()

    def stat_copy(src, dst, to):
        return remote(src, dst, "stat", (), to)

    for other in others:
        to = place(*other)
        stat_copy(stats.at[to["seq"]], arrived.at[me], to).start()
    everyone = arrived.at[pl.ds(0, count - 1)]
    stat_all = stat_copy(everyone, everyone, place(*others[0]))
    stat_all.wait_recv()
    result = arrived[0]
    for i in range(1, count):
        result = result + arrived[i]
    total, moment, chosen = result[0:1], result[1:2], result[2:3]
    log_norm = softcap + jnp.log(total)
    out_ref[0:1, :] = chosen - log_norm
    out_ref[1:2, :] = log_norm - moment / total
    stat_all.wait_send()


def on_device(seqs, vocabs, hidden, norm_gain, unembed, targets):
    rows, width = unembed.shape
    own, part = hidden.shape
    Y = 2 ** ((vocabs.bit_length() - 1) // 2)
    X, Z = seqs // CORES, vocabs // Y
    sizes = {"x": X, "y": Y, "z": Z}
    count = seqs * vocabs
    tokens = seqs * own
    tile = divisor(rows, 1600)
    sub = divisor(tile, 160)
    passes = plan(Z, Y, part)
    deepest = max(sum(piece[2] for piece in pieces) for pieces in passes)
    most = max(len(pieces) for pieces in passes)
    wide = divisor(rows, 4000)
    wide_sub = divisor(wide, 160)
    spare = width + chunk_gap(passes)
    planes = X * Y
    dma = pltpu.SemaphoreType.DMA
    vmem = pl.BlockSpec(memory_space=pltpu.VMEM)
    hbm = pl.BlockSpec(memory_space=pltpu.HBM)
    out = pl.pallas_call(
        functools.partial(head_kernel, sizes, tile, sub, wide, wide_sub),
        out_shape=jax.ShapeDtypeStruct((2, own), jnp.float32),
        in_specs=[hbm] * 4,
        out_specs=vmem,
        scratch_shapes=[
            pltpu.VMEM((CORES, Z, X, Y, part, own), jnp.bfloat16),
            pltpu.VMEM((width // LANES, LANES), jnp.float32),
            pltpu.VMEM((1, own), jnp.int32),
            pltpu.VMEM((width, LANES), jnp.float32),
            pltpu.VMEM((spare, tokens), jnp.bfloat16),
            pltpu.VMEM((count, 1, own), jnp.float32),
            pltpu.VMEM((seqs, 1, own), jnp.float32),
            pltpu.VMEM((seqs, 1, own), jnp.int32),
            pltpu.VMEM((SLOTS, tile, deepest), jnp.bfloat16),
            pltpu.VMEM((min(2, rows // wide), wide, passes[0][0][2]), jnp.bfloat16),
            pltpu.VMEM((rows, tokens), jnp.float32),
            pltpu.VMEM((3, 8, tokens), jnp.float32),
            pltpu.VMEM((seqs, 3, own), jnp.float32),
            pltpu.VMEM((count, 3, own), jnp.float32),
            {
                "square": dma((2,)),
                "target": dma((2, seqs)),
                "plane": dma((2, Z, planes)),
                "column": dma((2, Z)),
                "pair": dma((2, Z, planes)),
                "stat": dma((2,)),
            },
            dma((SLOTS, most)),
            dma((2,)),
            dma((3,)),
        ],
        compiler_params=pltpu.CompilerParams(
            collective_id=0, has_side_effects=True, vmem_limit_bytes=67000000
        ),
        name="head",
    )(hidden.T, norm_gain.reshape(width // LANES, LANES), targets.reshape(1, own), unembed)
    return out[0], out[1]


def solution(mesh):
    return jax.shard_map(
        functools.partial(on_device, mesh.shape["seq"], mesh.shape["vocab"]),
        mesh=mesh,
        in_specs=(P("seq", "vocab"), P(), P(("seq", "vocab"), None), P("seq")),
        out_specs=(P("seq"), P("seq")),
        check_vma=False,
    )
```

time: 78.1 us -> 68.8 us (0.88)
  Pallas kernels: 74.4 us -> 66.8 us
  local copies, waits for them, and re-layouts: 2.94 us -> 1.25 us
    pallas_call x1, Pallas kernels: 74.4 us -> 66.8 us  [on_device(): pl.pallas_call(functools.partial(head_kernel, sizes, tile, sub, wide, wid...]
    unnamed x1 -> x0, local copies, waits for them, and re-layouts: 1.71 us -> none
where the time goes in v2:
time: 68.8 us; the launch traced here: 68.7 us
  Pallas kernels  66.8 us (97%)
  local copies, waits for them, and re-layouts  1.25 us (2%)
    pallas_call x1, Pallas kernels, on_device(): pl.pallas_call(functools.partial(head_kernel, sizes, tile, sub, wide, wid...  66.8 us

profile of v2, /device:TPU:0, one launch (start us, length us, event | category | flops | bytes accessed | tf_op | source)
XLA Modules:
  0.0 68.7 jit_solution(11926676889663779154)
XLA Ops:
  0.6 66.8 %head.1 = f32[2,128]{1,0:T(2,128)} custom-call(bf16[576,128]{1,0:T(8,128)(2,1)} %bitcast.7, f32[36,128]{1,0:T(8,128)} %bitcast.8, s32[1,128]{1,0:T(1,128)} %bitcast.9, bf16[8000,4608]{1,0:T(8,128)(2,1)} %unembed_ref.1), custom_call_target="tpu_custom_call" | custom-call | tf_op jit(solution)/shard_map/head/pallas_call | solution.py:409
  67.4 1.3 %slice_bitcast_fusion = (f32[128]{0:T(128)}, f32[128]{0:T(128)}) fusion(f32[2,128]{1,0:T(2,128)} %head.1), kind=kLoop, calls=%fused_computation | loop fusion | bytes 2048 | tf_op jit(solution)/shard_map/squeeze | solution.py:446

commit v3 on v2

--- a/solution.py
+++ b/solution.py
@@ -13,7 +13,8 @@
 CORES = 2
 LANES = 128
 DEPTH = 256
-SLOTS = 3
+EARLY = 18
+LATE = 22
 MESH = pl.DeviceIdType.MESH
 
 
@@ -45,9 +46,9 @@
     return sum(piece[2] for pieces in passes for piece in pieces if piece[1] == "left")
 
 
-def head_kernel(sizes, tile, sub, wide, wide_sub, hidden_ref, gain_hbm, targets_hbm, unembed_ref, out_ref,
-                held, gain_ref, targets_ref, gains, normed, partial, scales, all_targets, weights, wides, logits, sums,
-                stats, arrived, sems, weight_sem, wide_sem, load_sem):
+def head_kernel(sizes, tile, sub, hidden_ref, gain_hbm, targets_hbm, unembed_ref, out_ref,
+                held, gain_ref, targets_ref, gains, normed, partial, scales, all_targets, weights, logits, sums,
+                stats, arrived, sems, weight_sem, load_sem):
     X, Y, Z = sizes["x"], sizes["y"], sizes["z"]
     seq, vocab = lax.axis_index("seq"), lax.axis_index("vocab")
     core = lax.rem(seq, CORES)
@@ -61,8 +62,8 @@
     passes = plan(Z, Y, part)
     split = [piece[1] for pieces in passes for piece in pieces].count("left") > 0
     halves = 2 if split else 1
-    narrow, tiles, broad = passes[halves:], rows // tile, rows // wide
-    total_steps = len(narrow) * tiles
+    tiles, slots = rows // tile, weights.shape[0]
+    last_pass = len(passes) - 1
     lead = passes[0][0][2]
     rest = chunk - lead
 
@@ -99,18 +100,10 @@
         behind = (1 - y) * lead
         return {"own": y * rest, "rest": behind, "left": behind + lead}.get(kind, 0)
 
-    def wide_fetch(p, i):
-        column = pl.multiple_of(level(0) * chunk + first_of(passes[p][0][1]), LANES)
-        slot = i % wides.shape[0]
-        return pltpu.make_async_copy(
-            unembed_ref.at[pl.ds(i * wide, wide), pl.ds(column, lead)],
-            wides.at[slot], wide_sem.at[slot],
-        )
-
     def fetches(p, i, slot):
         start, out = 0, []
         row = pl.ds(pl.multiple_of(i * tile, tile), tile)
-        for n, (k, first, length) in enumerate(narrow[p]):
+        for n, (k, first, length) in enumerate(passes[p]):
             column = pl.multiple_of(level(k) * chunk + first_of(first), LANES)
             out.append(pltpu.make_async_copy(
                 unembed_ref.at[row, pl.ds(column, length)],
@@ -120,12 +113,14 @@
             start += length
         return out
 
-    bulk = [(p, i) for p in range(halves) for i in range(broad)]
-    for p, i in bulk[:wides.shape[0]]:
-        wide_fetch(p, i).start()
-    for g in range(min(SLOTS - 1, total_steps)):
-        for copy in fetches(g // tiles, g % tiles, g % SLOTS):
+    def fetch(p, i, slot):
+        for copy in fetches(p, i, slot):
             copy.start()
+
+    bulk = [(p, i) for p in range(halves) for i in range(tiles)]
+    ahead = [(p, i) for p in range(len(passes)) for i in range(tiles)]
+    for n in range(min(slots, len(ahead))):
+        fetch(*ahead[n], n % slots)
 
     for load in loads:
         load.wait()
@@ -213,6 +208,9 @@
     for j in range(lanes):
         gains[j * LANES:(j + 1) * LANES, :] = jnp.broadcast_to(columns[:, j:j + 1], (LANES, LANES))
 
+    plane_arrived(0, near)
+    if Z > 1:
+        column_arrived(1)
     square_all.wait_recv()
     for s in range(seqs):
         squares = partial[s * vocabs]
@@ -240,9 +238,6 @@
     def far_arrived():
         plane_arrived(0, far)
 
-    plane_arrived(0, near)
-    if Z > 1:
-        column_arrived(1)
     pair_arrived(0, near + [len(peers)])
     normalize(0, (0,))
     if not split:
@@ -255,24 +250,28 @@
     sums[...] = jnp.zeros_like(sums)
 
     for n, (p, i) in enumerate(bulk):
-        slot = i % wides.shape[0]
+        slot = n % slots
         if split and (p, i) == (1, 0):
             pair_arrived(0, far)
             normalize(0, range(1, Y))
             normed[chunk:chunk + gap, :] = normed[
                 pl.ds(pl.multiple_of(first_of("left"), 16), gap), :
             ]
-        wide_fetch(p, i).wait()
+        for copy in fetches(p, i, slot):
+            copy.wait()
         start = pl.multiple_of(first_of(passes[p][0][1]), 16)
-        for s in range(wide // wide_sub):
-            here = pl.ds(i * wide + s * wide_sub, wide_sub)
+        for s in range(tile // sub):
+            if Z > 1 and n == len(bulk) - 1 and s == min(EARLY, tile // sub - 1):
+                last = far[-1:] if len(bulk) > 3 else near + far
+                plane_arrived(1, last)
+            here = pl.ds(i * tile + s * sub, sub)
             value = jnp.dot(
-                wides[slot, s * wide_sub:(s + 1) * wide_sub, :], normed[pl.ds(start, lead), :],
+                weights[slot, s * sub:(s + 1) * sub, 0:lead], normed[pl.ds(start, lead), :],
                 preferred_element_type=jnp.float32,
             )
             logits[here, :] = logits[here, :] + value if p else value
-        if n + wides.shape[0] < len(bulk):
-            wide_fetch(*bulk[n + wides.shape[0]]).start()
+        if n + slots < len(ahead):
+            fetch(*ahead[n + slots], slot)
         if split and n == 0:
             far_arrived()
         if n == min(1, len(bulk) - 1):
@@ -280,23 +279,24 @@
                 column_copy(k, z).start()
         if n == min(2, len(bulk) - 1) and Z > 2:
             column_arrived(2)
-        if n == min(2, len(bulk) - 1) and Z > 1:
-            plane_arrived(1, near)
-    if Z > 1:
-        plane_arrived(1, far)
+        if n == 2 and len(bulk) > 3 and Z > 1:
+            plane_arrived(1, near + far[:-1])
 
     def fold(values):
         return jnp.sum(values.reshape(sub // 8, 8, tokens), axis=0)
 
-    events = [[] for _ in narrow]
-    last_pass = len(narrow) - 1
+    subs = tile // sub
+    first = halves
+    events = {}
     for k in range(3, Z):
-        events[0].append((0, functools.partial(column_arrived, k)))
-    for n, k in enumerate(range(2, Z)):
-        events[0].append((min(tiles - 2 + n, tiles - 1), functools.partial(plane_arrived, k)))
+        events.setdefault((first, 0, 0), []).append(functools.partial(column_arrived, k))
+    for k in range(2, Z):
+        at = (first, tiles - 1, 0 if k < Z - 1 else min(LATE, subs - 1))
+        events.setdefault(at, []).append(functools.partial(plane_arrived, k))
 
     base = chunk if split else lead
-    for p, pieces in enumerate(narrow):
+    for p in range(halves, len(passes)):
+        pieces = passes[p]
         depth = sum(length for _, _, length in pieces)
         for k in sorted({piece[0] for piece in pieces}):
             if k:
@@ -304,27 +304,16 @@
                 normalize(k)
 
         def step(i, _, p=p, depth=depth, base=base):
-            g = p * tiles + i
-            slot = lax.rem(g, SLOTS)
-            ahead = lax.rem(g + SLOTS - 1, SLOTS)
-
-            def prefetch(q, n):
-                for copy in fetches(q, n, ahead):
-                    copy.start()
-
-            n = i + SLOTS - 1
-            for q in range(p, len(narrow)):
-                low, high = (q - p) * tiles, (q - p + 1) * tiles
-                if low > tiles - 1 + SLOTS - 1 or high <= SLOTS - 1:
-                    continue
-                pl.when((n >= low) & (n < high))(functools.partial(prefetch, q, n - low))
-            for at, event in events[p]:
-                pl.when(i == at)(event)
+            slot = lax.rem(p * tiles + i, slots)
             for copy in fetches(p, i, slot):
                 copy.wait()
             if p == last_pass:
                 total, moment, chosen = sums[0], sums[1], sums[2]
-            for s in range(tile // sub):
+            for s in range(subs):
+                for (q, turn, when), wanted in events.items():
+                    if (q, when) == (p, s):
+                        for event in wanted:
+                            pl.when(i == turn)(event)
                 here = pl.ds(pl.multiple_of(i * tile + s * sub, sub), sub)
                 value = jnp.dot(
                     weights[slot, s * sub:(s + 1) * sub, 0:depth], normed[base:base + depth, :],
@@ -342,6 +331,12 @@
                     chosen = chosen + fold(jnp.where(hit, squashed, 0.0))
             if p == last_pass:
                 sums[0], sums[1], sums[2] = total, moment, chosen
+            for q in range(p, len(passes)):
+                low = (q - p) * tiles - slots
+                if low < tiles and low + tiles > 0:
+                    pl.when((i >= low) & (i < low + tiles))(
+                        functools.partial(fetch, q, i - low, slot)
+                    )
             return 0
 
         lax.fori_loop(0, tiles, step, 0)
@@ -394,20 +389,19 @@
     sizes = {"x": X, "y": Y, "z": Z}
     count = seqs * vocabs
     tokens = seqs * own
-    tile = divisor(rows, 1600)
+    tile = divisor(rows, 4000)
     sub = divisor(tile, 160)
+    slots = min(2, rows // tile)
     passes = plan(Z, Y, part)
     deepest = max(sum(piece[2] for piece in pieces) for pieces in passes)
     most = max(len(pieces) for pieces in passes)
-    wide = divisor(rows, 4000)
-    wide_sub = divisor(wide, 160)
     spare = width + chunk_gap(passes)
     planes = X * Y
     dma = pltpu.SemaphoreType.DMA
     vmem = pl.BlockSpec(memory_space=pltpu.VMEM)
     hbm = pl.BlockSpec(memory_space=pltpu.HBM)
     out = pl.pallas_call(
-        functools.partial(head_kernel, sizes, tile, sub, wide, wide_sub),
+        functools.partial(head_kernel, sizes, tile, sub),
         out_shape=jax.ShapeDtypeStruct((2, own), jnp.float32),
         in_specs=[hbm] * 4,
         out_specs=vmem,
@@ -420,8 +414,7 @@
             pltpu.VMEM((count, 1, own), jnp.float32),
             pltpu.VMEM((seqs, 1, own), jnp.float32),
             pltpu.VMEM((seqs, 1, own), jnp.int32),
-            pltpu.VMEM((SLOTS, tile, deepest), jnp.bfloat16),
-            pltpu.VMEM((min(2, rows // wide), wide, passes[0][0][2]), jnp.bfloat16),
+            pltpu.VMEM((slots, tile, deepest), jnp.bfloat16),
             pltpu.VMEM((rows, tokens), jnp.float32),
             pltpu.VMEM((3, 8, tokens), jnp.float32),
             pltpu.VMEM((seqs, 3, own), jnp.float32),
@@ -434,8 +427,7 @@
                 "pair": dma((2, Z, planes)),
                 "stat": dma((2,)),
             },
-            dma((SLOTS, most)),
-            dma((2,)),
+            dma((slots, most)),
             dma((3,)),
         ],
         compiler_params=pltpu.CompilerParams(

time: 68.8 us -> 66.5 us (0.967)
  Pallas kernels: 66.8 us -> 64.5 us
    pallas_call x1, Pallas kernels: 66.8 us -> 64.5 us  [on_device(): pl.pallas_call(functools.partial(head_kernel, sizes, tile, sub), out_shap...]
where the time goes in v3:
time: 66.5 us; the launch traced here: 66.4 us
  Pallas kernels  64.5 us (97%)
  local copies, waits for them, and re-layouts  1.25 us (2%)
    pallas_call x1, Pallas kernels, on_device(): pl.pallas_call(functools.partial(head_kernel, sizes, tile, sub), out_shap...  64.5 us

profile of v3, /device:TPU:0, one launch (start us, length us, event | category | flops | bytes accessed | tf_op | source)
XLA Modules:
  0.0 66.4 jit_solution(15279016830002889992)
XLA Ops:
  0.6 64.5 %head.1 = f32[2,128]{1,0:T(2,128)} custom-call(bf16[576,128]{1,0:T(8,128)(2,1)} %bitcast.7, f32[36,128]{1,0:T(8,128)} %bitcast.8, s32[1,128]{1,0:T(1,128)} %bitcast.9, bf16[8000,4608]{1,0:T(8,128)(2,1)} %unembed_ref.1), custom_call_target="tpu_custom_call" | custom-call | tf_op jit(solution)/shard_map/head/pallas_call | solution.py:403
  65.1 1.3 %slice_bitcast_fusion = (f32[128]{0:T(128)}, f32[128]{0:T(128)}) fusion(f32[2,128]{1,0:T(2,128)} %head.1), kind=kLoop, calls=%fused_computation | loop fusion | bytes 2048 | tf_op jit(solution)/shard_map/squeeze | solution.py:438
